TPU v7x, 32 devices: a whole 2x2x4 slice. The times are simulated.
32 devices in a mesh: rep: 16 (over z, x, core), slab: 2 (over y).
Axes of the slice: x: 2, y: 2, z: 4, core: 2. Of those that a mesh axis runs over, the one named last changes fastest.
Arguments:
- weights: bfloat16 [16, 256, 3072], P('rep', 'slab'), may hold values from -6 to 6
- perms: int32 [16, 8, 256], P('rep'), may hold values from 0 to 255, each once within a row
Outputs:
- merged: bfloat16 [16, 256, 3072], P('rep', 'slab')
Inputs may be any that keep to these rules, and one draw needn't show every extreme that they name: `perms`: each row of 256 entries names every neuron of the window once.
All inputs are finite; a program needn't handle non-finite values.
Results may differ from a plain program's by a relative error of at most 0.012.
Values may be sent and summed in bfloat16 or wider, within the bound.
A program may use at most 64 MiB of HBM per device.

v0:
```python
import functools
import math

import jax
import jax.numpy as jnp
from jax import lax
from jax.experimental import pallas as pl
from jax.experimental.pallas import tpu as pltpu
from jax.sharding import PartitionSpec as P

CHUNK = 256
PIECES = 2


def placements(bits, rounds):
    position = {b: b for b in range(1, bits)}
    plan = [(0, None, dict(position))]
    for r in range(1, rounds):
        old, new = (r - 1) % bits, r % bits
        device_bit = position.pop(new)
        position[old] = device_bit
        plan.append((new, device_bit, dict(position)))
    return plan


def kernel(n_rep, n_slab, rounds, w_ref, p_ref, out_ref,
           state, sent, kept, part, core_in, slab_out, slab_in, cost_ref, perms, hot,
           in_send, in_recv, ex_send, ex_recv, core_send, core_recv, slab_send, slab_recv,
           cost_send, cost_recv, out_send, out_recv, perm_send, perm_recv):
    bits = n_rep.bit_length() - 1
    me = lax.axis_index("rep")
    slab = lax.axis_index("slab")
    core = me % 2
    half, width = w_ref.shape[1], w_ref.shape[2]
    ffw = half * n_slab
    block = width // (2 * n_slab)
    chunks = block // CHUNK
    plan = placements(bits, rounds)

    def bit(b):
        return (me // (1 << b)) % 2

    def flipped(b):
        return me + (1 - 2 * bit(b)) * (1 << b)

    def remote(src, dst, send, recv, rep_to, slab_to):
        return pltpu.make_async_remote_copy(
            src_ref=src, dst_ref=dst, send_sem=send, recv_sem=recv,
            device_id=(rep_to, slab_to), device_id_type=pl.DeviceIdType.MESH)

    barrier = pltpu.get_barrier_semaphore()
    devices = n_rep * n_slab

    def greet(k, carry):
        to = lax.rem(me * n_slab + slab + k, devices)
        pl.semaphore_signal(barrier, inc=1, device_id=(to // n_slab, to % n_slab),
                            device_id_type=pl.DeviceIdType.MESH)
        return carry

    lax.fori_loop(1, devices, greet, 0)
    pl.semaphore_wait(barrier, devices - 1)

    first_waits = []
    rows_here = pl.ds(pl.multiple_of(slab * half, half), half)
    for k in range(chunks):
        for ds_ in range(n_slab):
            for dc in range(2):
                rep_to = me if dc == 0 else flipped(0)
                core_to = core if dc == 0 else 1 - core
                slab_to = (slab + ds_) % n_slab
                start = (slab_to * 2 + core_to) * block + k * CHUNK
                src = w_ref.at[0, :, pl.ds(pl.multiple_of(start, CHUNK), CHUNK)]
                dst = state.at[core, k, rows_here]
                if ds_ == 0 and dc == 0:
                    copy = pltpu.make_async_copy(src, dst, in_recv.at[0, 0, k])
                else:
                    copy = remote(src, dst, in_send.at[ds_, dc, k], in_recv.at[ds_, dc, k], rep_to, slab_to)
                copy.start()
                first_waits.append((k, copy))

    perms[me] = p_ref[0]

    def spread(k, carry):
        to = lax.rem(me + k, n_rep)
        remote(p_ref.at[0], perms.at[me], perm_send, perm_recv, to, slab).start()
        return carry

    lax.fori_loop(1, n_rep, spread, 0)
    others = perms.at[pl.ds(0, n_rep - 1)]
    spread_all = remote(others, others, perm_send, perm_recv, flipped(0), slab)

    def contribution(a, b):
        return lax.dot_general(a, b, (((1,), (1,)), ((), ())), preferred_element_type=jnp.float32)

    pending = []
    exchange = None
    for r in range(rounds):
        local_bit, device_bit, position = plan[r]
        last = r == rounds - 1

        mine = None if device_bit is None else bit(device_bit)
        stays = mine if last else bit(plan[r + 1][1])
        if r == 0:
            first, second = 1 - stays, stays
        else:
            same = 1 - (stays + mine) % 2 if not last else 1
            first, second = 2 * r + same, 2 * r + 1 - same
        base = 0
        for b, p in position.items():
            base = base + bit(p) * (1 << b)
        first_rep = base + (1 - stays) * (1 << local_bit)
        second_rep = base + stays * (1 << local_bit)

        partial = None
        for k in range(chunks):
            if r == 0:
                for at, copy in first_waits:
                    if at == k:
                        copy.wait()
            else:
                for piece in exchange:
                    piece[k].wait_recv()
            term = contribution(state[first, k], state[second, k])
            partial = term if partial is None else partial + term
        part[r] = partial.reshape(2, ffw // 2, ffw)
        quarter = ffw // 2 // PIECES
        to_cores = []
        for q in range(PIECES):
            its = pl.ds(q * quarter, quarter)
            copy = remote(part.at[r, 1 - core, its], core_in.at[r, its], core_send.at[r, q], core_recv.at[r, q],
                          flipped(0), slab)
            copy.start()
            to_cores.append(copy)
        if r == 0:
            spread_all.wait()
        columns = lax.broadcasted_iota(jnp.int32, (ffw, ffw), 1)
        rows = lax.broadcasted_iota(jnp.int32, (ffw, ffw), 0)
        first_perm = perms[first_rep].astype(jnp.float32).T[:, r:r + 1].astype(jnp.int32)
        second_perm = perms[second_rep, r:r + 1, :]
        first_hot = (first_perm == columns).astype(jnp.float32)
        second_hot = (second_perm == rows).astype(jnp.float32)
        to_slabs = []
        for q in range(PIECES):
            its = pl.ds(q * quarter, quarter)
            to_cores[q].wait_recv()
            total = part[r, core, its, :] + core_in[r, its, :]
            cost_ref[r, core, its, :] = total
            slab_out[r, its, :] = total.astype(slab_out.dtype)
            for ds_ in range(1, n_slab):
                copy = remote(slab_out.at[r, its], slab_in.at[r, ds_ - 1, its], slab_send.at[r, ds_ - 1, q],
                              slab_recv.at[r, ds_ - 1, q], me, (slab + ds_) % n_slab)
                copy.start()
                to_slabs.append(copy)
        to_costs = []
        pending += to_cores + to_slabs

        scale = 1.0 / math.sqrt(width)
        half_rows = ffw // 2
        row_sets = [pl.ds(pl.multiple_of(core * half_rows + q * quarter, quarter), quarter) for q in range(PIECES)]
        row_sets += [pl.ds(pl.multiple_of((1 - core) * half_rows + q * quarter, quarter), quarter)
                     for q in range(PIECES)]

        def merged(own, mix, other):
            aligned = 0.5 * jnp.dot(mix, other, preferred_element_type=jnp.float32)
            return ((own.astype(jnp.float32) + aligned) * (1.0 / math.sqrt(2.0))).astype(jnp.bfloat16)

        if last:
            source = slab * 2 + core

            def deliver(buffer, at, owner, h, k):
                column = source * block + k * CHUNK
                src = buffer.at[k, pl.ds(pl.multiple_of(h * half, half), half)]
                dst = out_ref.at[0, :, pl.ds(pl.multiple_of(column, CHUNK), CHUNK)]
                stay = jnp.logical_and(owner == me, slab == h)

                @pl.when(stay)
                def _():
                    pltpu.make_async_copy(src, dst, out_recv.at[source, k]).start()

                @pl.when(jnp.logical_not(stay))
                def _():
                    remote(src, dst, out_send.at[at, h, k], out_recv.at[source, k], owner, h).start()
        else:
            exchange = [[] for _ in row_sets]

        fourths = []
        for part_at, its_rows in enumerate(row_sets):
            q = part_at % PIECES
            its = pl.ds(q * quarter, quarter)
            if part_at < PIECES:
                total = cost_ref[r, core, its, :]
                for ds_ in range(1, n_slab):
                    to_slabs[q * (n_slab - 1) + ds_ - 1].wait_recv()
                    total = total + slab_in[r, ds_ - 1, its, :].astype(jnp.float32)
                cost_ref[r, core, its, :] = total
                copy = remote(cost_ref.at[r, core, its], cost_ref.at[r, core, its], cost_send.at[r, q],
                              cost_recv.at[r, q], flipped(0), slab)
                copy.start()
                to_costs.append(copy)
            else:
                to_costs[q].wait_recv()
                total = cost_ref[r, 1 - core, its, :]
            cost = total * scale
            squared = cost * cost
            fourth = squared * squared
            fourths.append(fourth)
            by_row = 1.0 / (1.0 + jnp.sum(fourth, axis=1, keepdims=True))
            if part_at == 0:
                hot[...] = first_hot
            mix = (hot[its_rows, :] + fourth * by_row).astype(jnp.bfloat16)
            for k in range(chunks):
                sent[r, k, its_rows, :] = merged(state[first, k, its_rows, :], mix, state[second, k])
                if not last:
                    copy = remote(sent.at[r, k, its_rows], state.at[2 * (r + 1) + 1, k, its_rows],
                                  ex_send.at[r, part_at, k], ex_recv.at[r, part_at, k],
                                  flipped(plan[r + 1][1]), slab)
                    copy.start()
                    exchange[part_at].append(copy)
                elif n_slab == 2 and q == PIECES - 1:
                    deliver(sent.at[r], 0, first_rep, core if part_at < PIECES else 1 - core, k)
            if last and n_slab != 2 and part_at == len(row_sets) - 1:
                for k in range(chunks):
                    for h in range(n_slab):
                        deliver(sent.at[r], 0, first_rep, h, k)
        by_column = 1.0 / (1.0 + sum(jnp.sum(f, axis=0, keepdims=True) for f in fourths))
        for f, its_rows in zip(fourths, row_sets):
            hot[its_rows, :] = f * by_column
        second_mix = (second_hot + hot[...]).T.astype(jnp.bfloat16)
        for k in range(chunks):
            new = merged(state[second, k], second_mix, state[first, k])
            if last:
                kept[k] = new
                for h in range(n_slab):
                    deliver(kept, 1, second_rep, h, k)
            else:
                state[2 * (r + 1), k] = new
        if not last:
            pending += sum(exchange, []) + to_costs
        else:
            pending += to_costs
            for k in range(chunks):
                for s in range(2 * n_slab):
                    dst = out_ref.at[0, :, pl.ds(s * block + k * CHUNK, CHUNK)]
                    pltpu.make_async_copy(dst, dst, out_recv.at[s, k]).wait()
                for at, owner, buffer in ((0, first_rep, sent.at[r]), (1, second_rep, kept)):
                    for h in range(n_slab):
                        @pl.when(jnp.logical_not(jnp.logical_and(owner == me, slab == h)))
                        def _():
                            src = buffer.at[k, pl.ds(h * half, half)]
                            dst = out_ref.at[0, :, pl.ds(k * CHUNK, CHUNK)]
                            remote(src, dst, out_send.at[at, h, k], out_recv.at[0, k], owner, h).wait_send()
    for copy in pending:
        copy.wait_send()


def solution(mesh):
    n_rep, n_slab = mesh.shape["rep"], mesh.shape["slab"]

    def local(weights, perms):
        _, half, width = weights.shape
        rounds = perms.shape[1]
        ffw = perms.shape[2]
        chunks = width // (2 * n_slab) // CHUNK
        vmem = pltpu.VMEM
        dma = pltpu.SemaphoreType.DMA
        bf16, f32 = jnp.bfloat16, jnp.float32
        return pl.pallas_call(
            functools.partial(kernel, n_rep, n_slab, rounds),
            out_shape=jax.ShapeDtypeStruct(weights.shape, weights.dtype),
            in_specs=[pl.BlockSpec(memory_space=pltpu.VMEM)] * 2,
            out_specs=pl.BlockSpec(memory_space=pltpu.VMEM),
            scratch_shapes=[
                vmem((2 * rounds, chunks, ffw, CHUNK), bf16),
                vmem((rounds, chunks, ffw, CHUNK), bf16),
                vmem((chunks, ffw, CHUNK), bf16),
                vmem((rounds, 2, ffw // 2, ffw), f32),
                vmem((rounds, ffw // 2, ffw), f32),
                vmem((rounds, ffw // 2, ffw), bf16),
                vmem((rounds, n_slab - 1, ffw // 2, ffw), bf16),
                vmem((rounds, 2, ffw // 2, ffw), f32),
                vmem((n_rep, rounds, ffw), jnp.int32),
                vmem((ffw, ffw), f32),
                dma((n_slab, 2, chunks)), dma((n_slab, 2, chunks)),
                dma((rounds, 2 * PIECES, chunks)), dma((rounds, 2 * PIECES, chunks)),
                dma((rounds, PIECES)), dma((rounds, PIECES)),
                dma((rounds, n_slab - 1, PIECES)), dma((rounds, n_slab - 1, PIECES)),
                dma((rounds, PIECES)), dma((rounds, PIECES)),
                dma((2, n_slab, chunks)), dma((2 * n_slab, chunks)),
                dma, dma,
            ],
            compiler_params=pltpu.CompilerParams(collective_id=0, has_side_effects=True, vmem_limit_bytes=60 * 1024 * 1024),
        )(weights, perms)

    return jax.shard_map(
        local, mesh=mesh, in_specs=(P("rep", "slab", None), P("rep", None, None)),
        out_specs=P("rep", "slab", None), check_vma=False,
    )
```

profile of v0, /device:TPU:28, one launch (start us, length us, event | category | flops | bytes accessed | tf_op | source)
XLA Modules:
  0.0 167.6 jit_solution(8494460703158365468)
XLA Ops:
  0.0 165.6 %shard_map.28 = bf16[1,128,3072]{2,1,0:T(8,128)(2,1)} custom-call(bf16[1,128,3072]{2,1,0:T(8,128)(2,1)} %w_ref.1, s32[1,8,256]{2,1,0:T(8,128)} %p_ref.1), custom_call_target="tpu_custom_call" | custom-call | tf_op jit(solution)/shard_map/pallas_call | solution.py:267
  165.6 2.1 %copy.4 = bf16[1,128,3072]{2,1,0:T(8,128)(2,1)} copy(bf16[1,128,3072]{2,1,0:T(8,128)(2,1)} %shard_map.28) | data formatting | bytes 1572864
where the time goes:
time: 168 us
  Pallas kernels  166 us (99%)
  local copies, waits for them, and re-layouts  2.06 us (1%)
    pallas_call x1, Pallas kernels, local(): pl.pallas_call(functools.partial(kernel, n_rep, n_slab, rounds), out_shap...  166 us

commit v1 on v0

v1 whole, which is shorter than its diff:
```python
import functools
import math

import jax
import jax.numpy as jnp
from jax import lax
from jax.experimental import pallas as pl
from jax.experimental.pallas import tpu as pltpu
from jax.sharding import PartitionSpec as P

CHUNK = 256
PIECES = 4
LAG = 2


def kernel(n_rep, n_slab, rounds, cuts, w_ref, p_ref, out_ref,
           init, vis, sent, part, core_in, half_out, half_in, fourths, hot_v, hot_r, perms, rows_v, cols_v,
           in_send, in_recv, ex_send, ex_recv, core_send, core_recv, half_send, half_recv,
           out_send, home_send, out_recv, perm_send, perm_recv):
    bits = n_rep.bit_length() - 1
    me = lax.axis_index("rep")
    slab = lax.axis_index("slab")
    core = me % 2
    half, width = w_ref.shape[1], w_ref.shape[2]
    ffw = half * n_slab
    block = width // (2 * n_slab)
    scale = 1.0 / math.sqrt(width)

    def bit(b):
        return (me // (1 << b)) % 2

    def flipped(*at):
        to = me
        for b in at:
            to = to + (1 - 2 * bit(b)) * (1 << b)
        return to

    odd = sum(bit(b) for b in range(bits)) % 2
    resident = me + odd * (1 - 2 * core)

    def remote(src, dst, send, recv, rep_to, slab_to):
        return pltpu.make_async_remote_copy(
            src_ref=src, dst_ref=dst, send_sem=send, recv_sem=recv,
            device_id=(rep_to, slab_to), device_id_type=pl.DeviceIdType.MESH)

    barrier = pltpu.get_barrier_semaphore()
    devices = n_rep * n_slab

    def greet(k, carry):
        to = lax.rem(me * n_slab + slab + k, devices)
        pl.semaphore_signal(barrier, inc=1, device_id=(to // n_slab, to % n_slab),
                            device_id_type=pl.DeviceIdType.MESH)
        return carry

    lax.fori_loop(1, devices, greet, 0)
    pl.semaphore_wait(barrier, devices - 1)

    firsts = []
    rows_here = pl.ds(pl.multiple_of(slab * half, half), half)
    for ds_ in list(range(1, n_slab)) + [0]:
        for dc in range(2):
            slab_to = (slab + ds_) % n_slab
            core_to = core if dc == 0 else 1 - core
            start = (slab_to * 2 + core_to) * block
            src = w_ref.at[0, :, pl.ds(pl.multiple_of(start, 128), block)]
            dst = init.at[odd, rows_here]
            if ds_ == 0 and dc == 0:
                copy = pltpu.make_async_copy(src, dst, in_recv.at[0, 0])
            else:
                copy = remote(src, dst, in_send.at[ds_, dc], in_recv.at[ds_, dc],
                              me if dc == 0 else flipped(0), slab_to)
            copy.start()
            firsts.append(copy)

    perms[0] = p_ref[0]
    for b in range(bits):
        for c in range(2):
            if 2 * b + c > 0:
                to = flipped(b) if c == 0 else (flipped(0, b) if b else flipped(0))
                remote(p_ref.at[0], perms.at[2 * b + c], perm_send, perm_recv, to, slab).start()
    others = perms.at[pl.ds(1, 2 * bits - 1)]
    spread_all = remote(others, others, perm_send, perm_recv, flipped(0), slab)

    for copy in firsts:
        copy.wait()

    def visitor_of(r):
        return init.at[1] if r == 0 else vis.at[r - 1]

    def merged(own, mix, other):
        aligned = 0.5 * jnp.dot(mix, other, preferred_element_type=jnp.float32)
        return ((own.astype(jnp.float32) + aligned) * (1.0 / math.sqrt(2.0))).astype(jnp.bfloat16)

    chunks = [pl.ds(k * CHUNK, CHUNK) for k in range(block // CHUNK)]
    spans = [pl.ds(a, b - a) for a, b in zip(cuts[:-1], cuts[1:])]
    columns = lax.broadcasted_iota(jnp.int32, (ffw, ffw), 1)
    rows = lax.broadcasted_iota(jnp.int32, (ffw, ffw), 0)

    def hots(r):
        hot_v[...] = (cols_v[:, r:r + 1].astype(jnp.int32) == columns).astype(jnp.float32)
        hot_r[...] = (perms[odd, r:r + 1, :] == rows).astype(jnp.float32)

    pending = []
    arrivals = None
    source = slab * 2 + core
    for r in range(rounds):
        last = r == rounds - 1
        visitor = visitor_of(r)
        sums = [[] for _ in spans]
        total_columns = [None]
        onward = []

        def cost(q):
            its = spans[q]
            if r:
                arrivals[q].wait_recv()
            partial = lax.dot_general(visitor[its, :], init[0], (((1,), (1,)), ((), ())),
                                      preferred_element_type=jnp.float32)
            part[r, its, :] = partial
            half_out[r, its, :] = partial.astype(half_out.dtype)
            for ds_ in range(1, n_slab):
                for dc in range(2):
                    at = 2 * (ds_ - 1) + dc
                    sums[q].append(remote(half_out.at[r, its], half_in.at[r, at, its], half_send.at[r, at, q],
                                          half_recv.at[r, at, q], me if dc == 0 else flipped(0),
                                          (slab + ds_) % n_slab))
            sums[q].append(remote(part.at[r, its], core_in.at[r, its], core_send.at[r, q], core_recv.at[r, q],
                                  flipped(0), slab))
            for copy in sums[q]:
                copy.start()

        def finish(q):
            its = spans[q]
            for copy in sums[q]:
                copy.wait_recv()
            total = part[r, its, :] + core_in[r, its, :]
            for at in range(2 * (n_slab - 1)):
                total = total + half_in[r, at, its, :].astype(jnp.float32)
            scaled = total * scale
            squared = scaled * scaled
            fourth = squared * squared
            fourths[its, :] = fourth
            by_row = 1.0 / (1.0 + jnp.sum(fourth, axis=1, keepdims=True))
            mix = (hot_v[its, :] + fourth * by_row).astype(jnp.bfloat16)
            for k in chunks:
                sent[r, its, k] = merged(visitor[its, k], mix, init[0, :, k])
            if last:
                h = cuts[q] // half
                dst = out_ref.at[0, pl.ds(cuts[q] - h * half, cuts[q + 1] - cuts[q]),
                                 pl.ds(pl.multiple_of(source * block, 128), block)]
                j = resident_flipped(r % bits)
                copy = remote(sent.at[r, its], dst, out_send.at[q], out_recv.at[source], j, h)
            else:
                copy = remote(sent.at[r, its], vis.at[r, its], ex_send.at[r, q], ex_recv.at[r, q],
                              flipped(*[b for b in (r % bits, (r + 1) % bits) if b]), slab)
            copy.start()
            onward.append(copy)
            by_columns = jnp.sum(fourth, axis=0, keepdims=True)
            total_columns[0] = by_columns if total_columns[0] is None else total_columns[0] + by_columns

        def resident_flipped(b):
            if b == 0:
                return me + (1 - odd) * (1 - 2 * core)
            return resident + (1 - 2 * bit(b)) * (1 << b)

        lag = len(spans) if r == 0 else LAG
        for q in range(len(spans) + lag):
            if q < len(spans):
                cost(q)
            if r == 0 and q == len(spans) - 1:
                spread_all.wait()
                for s in range(rounds):
                    b = s % bits
                    rows_v[s:s + 1, :] = (perms[2 * b + odd, s:s + 1, :] if b else
                                          perms[1 - odd, s:s + 1, :]).astype(jnp.float32)
                cols_v[...] = rows_v[...].T
                hots(0)
            if q >= lag:
                finish(q - lag)

        by_column = 1.0 / (1.0 + total_columns[0])
        mix = (hot_r[...] + fourths[...] * by_column).astype(jnp.bfloat16).T
        for k in chunks:
            init[0, :, k] = merged(init[0, :, k], mix, visitor[:, k])
        pending += sum(sums, [])
        arrivals = onward
        if last:
            for h in range(n_slab):
                src = init.at[0, pl.ds(h * half, half)]
                dst = out_ref.at[0, :, pl.ds(pl.multiple_of(source * block, 128), block)]
                stay = jnp.logical_and(odd == 0, slab == h)

                @pl.when(stay)
                def _():
                    pltpu.make_async_copy(src, dst, out_recv.at[source]).start()

                @pl.when(jnp.logical_not(stay))
                def _():
                    remote(src, dst, home_send.at[h], out_recv.at[source], resident, h).start()
            for copy in onward:
                copy.wait_send()
            for h in range(n_slab):
                stay = jnp.logical_and(odd == 0, slab == h)

                @pl.when(jnp.logical_not(stay))
                def _():
                    src = init.at[0, pl.ds(h * half, half)]
                    dst = out_ref.at[0, :, pl.ds(0, block)]
                    remote(src, dst, home_send.at[h], out_recv.at[0], resident, h).wait_send()
            for s in range(2 * n_slab):
                dst = out_ref.at[0, :, pl.ds(s * block, block)]
                pltpu.make_async_copy(dst, dst, out_recv.at[s]).wait()
        else:
            pending += onward
            hots(r + 1)
    for copy in pending:
        copy.wait_send()


def solution(mesh):
    n_rep, n_slab = mesh.shape["rep"], mesh.shape["slab"]

    def local(weights, perms):
        _, half, width = weights.shape
        rounds = perms.shape[1]
        ffw = perms.shape[2]
        bits = n_rep.bit_length() - 1
        block = width // (2 * n_slab)
        size = ffw // PIECES
        cuts = list(range(0, ffw + 1, size))
        pieces = len(cuts) - 1
        vmem = pltpu.VMEM
        dma = pltpu.SemaphoreType.DMA
        bf16, f32 = jnp.bfloat16, jnp.float32
        away = 2 * (n_slab - 1)
        return pl.pallas_call(
            functools.partial(kernel, n_rep, n_slab, rounds, cuts),
            out_shape=jax.ShapeDtypeStruct(weights.shape, weights.dtype),
            in_specs=[pl.BlockSpec(memory_space=pltpu.VMEM)] * 2,
            out_specs=pl.BlockSpec(memory_space=pltpu.VMEM),
            scratch_shapes=[
                vmem((2, ffw, block), bf16),
                vmem((rounds - 1, ffw, block), bf16),
                vmem((rounds, ffw, block), bf16),
                vmem((rounds, ffw, ffw), f32),
                vmem((rounds, ffw, ffw), f32),
                vmem((rounds, ffw, ffw), bf16),
                vmem((rounds, away, ffw, ffw), bf16),
                vmem((ffw, ffw), f32),
                vmem((ffw, ffw), f32),
                vmem((ffw, ffw), f32),
                vmem((2 * bits, rounds, ffw), jnp.int32),
                vmem((rounds, ffw), f32),
                vmem((ffw, rounds), f32),
                dma((n_slab, 2)), dma((n_slab, 2)),
                dma((rounds, pieces)), dma((rounds, pieces)),
                dma((rounds, pieces)), dma((rounds, pieces)),
                dma((rounds, away, pieces)), dma((rounds, away, pieces)),
                dma((pieces,)), dma((n_slab,)), dma((2 * n_slab,)),
                dma, dma,
            ],
            compiler_params=pltpu.CompilerParams(collective_id=0, has_side_effects=True, vmem_limit_bytes=60 * 1024 * 1024),
        )(weights, perms)

    return jax.shard_map(
        local, mesh=mesh, in_specs=(P("rep", "slab", None), P("rep", None, None)),
        out_specs=P("rep", "slab", None), check_vma=False,
    )
```

time: 168 us -> 136 us (0.81)
  the two profiles are of different devices: /device:TPU:28 before, /device:TPU:9 now
where the time goes in v1:
time: 136 us
  Pallas kernels  134 us (99%)
  local copies, waits for them, and re-layouts  2.06 us (2%)
    pallas_call x1, Pallas kernels, local(): pl.pallas_call(functools.partial(kernel, n_rep, n_slab, rounds, cuts), ou...  134 us

profile of v1, /device:TPU:9, one launch (start us, length us, event | category | flops | bytes accessed | tf_op | source)
XLA Modules:
  0.0 135.8 jit_solution(5539736651982945537)
XLA Ops:
  0.0 133.8 %shard_map.28 = bf16[1,128,3072]{2,1,0:T(8,128)(2,1)} custom-call(bf16[1,128,3072]{2,1,0:T(8,128)(2,1)} %w_ref.1, s32[1,8,256]{2,1,0:T(8,128)} %p_ref.1), custom_call_target="tpu_custom_call" | custom-call | tf_op jit(solution)/shard_map/pallas_call | solution.py:236
  133.8 2.1 %copy.4 = bf16[1,128,3072]{2,1,0:T(8,128)(2,1)} copy(bf16[1,128,3072]{2,1,0:T(8,128)(2,1)} %shard_map.28) | data formatting | bytes 1572864

commit v2 on v1

--- a/solution.py
+++ b/solution.py
@@ -13,9 +13,13 @@
 LAG = 2
 
 
-def kernel(n_rep, n_slab, rounds, cuts, w_ref, p_ref, out_ref,
-           init, vis, sent, part, core_in, half_out, half_in, fourths, hot_v, hot_r, perms, rows_v, cols_v,
-           in_send, in_recv, ex_send, ex_recv, core_send, core_recv, half_send, half_recv,
+def moves(r, bits):
+    return tuple(sorted(b for b in ((r - 1) % bits, r % bits) if b))
+
+
+def kernel(n_rep, n_slab, rounds, cuts, w_hbm, p_hbm, out_ref,
+           w_ref, p_ref, init, vis, sent, part, core_in, half_out, half_in, fourths, hot_v, hot_r, perms, rows_v, cols_v,
+           load, in_send, in_recv, ex_send, ex_recv, core_send, core_recv, half_send, half_recv,
            out_send, home_send, out_recv, perm_send, perm_recv):
     bits = n_rep.bit_length() - 1
     me = lax.axis_index("rep")
@@ -43,17 +47,24 @@
             src_ref=src, dst_ref=dst, send_sem=send, recv_sem=recv,
             device_id=(rep_to, slab_to), device_id_type=pl.DeviceIdType.MESH)
 
+    loads = [pltpu.make_async_copy(p_hbm, p_ref, load.at[0]), pltpu.make_async_copy(w_hbm, w_ref, load.at[1])]
+    for copy in loads:
+        copy.start()
+
+    near = {(0,)} | {tuple(sorted({0, b} - {0} | extra)) for b in range(1, bits) for extra in ({0}, set())}
+    for r in range(1, rounds):
+        near.add(moves(r, bits))
+    final = (rounds - 1) % bits
+    across = {(), (0,), tuple({final} - {0}), tuple(sorted({0, final}))}
+    peers = [(at, 0) for at in sorted(near | across) if at]
+    peers += [(at, ds_) for ds_ in range(1, n_slab) for at in sorted(across)]
     barrier = pltpu.get_barrier_semaphore()
-    devices = n_rep * n_slab
-
-    def greet(k, carry):
-        to = lax.rem(me * n_slab + slab + k, devices)
-        pl.semaphore_signal(barrier, inc=1, device_id=(to // n_slab, to % n_slab),
+    for at, ds_ in peers:
+        pl.semaphore_signal(barrier, inc=1, device_id=(flipped(*at), (slab + ds_) % n_slab),
                             device_id_type=pl.DeviceIdType.MESH)
-        return carry
-
-    lax.fori_loop(1, devices, greet, 0)
-    pl.semaphore_wait(barrier, devices - 1)
+    pl.semaphore_wait(barrier, len(peers))
+    for copy in loads:
+        copy.wait()
 
     firsts = []
     rows_here = pl.ds(pl.multiple_of(slab * half, half), half)
@@ -81,9 +92,6 @@
     others = perms.at[pl.ds(1, 2 * bits - 1)]
     spread_all = remote(others, others, perm_send, perm_recv, flipped(0), slab)
 
-    for copy in firsts:
-        copy.wait()
-
     def visitor_of(r):
         return init.at[1] if r == 0 else vis.at[r - 1]
 
@@ -96,9 +104,16 @@
     columns = lax.broadcasted_iota(jnp.int32, (ffw, ffw), 1)
     rows = lax.broadcasted_iota(jnp.int32, (ffw, ffw), 0)
 
-    def hots(r):
-        hot_v[...] = (cols_v[:, r:r + 1].astype(jnp.int32) == columns).astype(jnp.float32)
-        hot_r[...] = (perms[odd, r:r + 1, :] == rows).astype(jnp.float32)
+    spread_all.wait()
+    for r in range(rounds):
+        b = r % bits
+        rows_v[r:r + 1, :] = (perms[2 * b + odd, r:r + 1, :] if b else perms[1 - odd, r:r + 1, :]).astype(jnp.float32)
+    cols_v[...] = rows_v[...].T
+    for r in range(rounds):
+        hot_v[r] = (cols_v[:, r:r + 1].astype(jnp.int32) == columns).astype(jnp.float32)
+        hot_r[r] = (perms[odd, r:r + 1, :] == rows).astype(jnp.float32)
+    for copy in firsts:
+        copy.wait()
 
     pending = []
     arrivals = None
@@ -141,7 +156,7 @@
             fourth = squared * squared
             fourths[its, :] = fourth
             by_row = 1.0 / (1.0 + jnp.sum(fourth, axis=1, keepdims=True))
-            mix = (hot_v[its, :] + fourth * by_row).astype(jnp.bfloat16)
+            mix = (hot_v[r, its, :] + fourth * by_row).astype(jnp.bfloat16)
             for k in chunks:
                 sent[r, its, k] = merged(visitor[its, k], mix, init[0, :, k])
             if last:
@@ -152,7 +167,7 @@
                 copy = remote(sent.at[r, its], dst, out_send.at[q], out_recv.at[source], j, h)
             else:
                 copy = remote(sent.at[r, its], vis.at[r, its], ex_send.at[r, q], ex_recv.at[r, q],
-                              flipped(*[b for b in (r % bits, (r + 1) % bits) if b]), slab)
+                              flipped(*moves(r + 1, bits)), slab)
             copy.start()
             onward.append(copy)
             by_columns = jnp.sum(fourth, axis=0, keepdims=True)
@@ -163,23 +178,15 @@
                 return me + (1 - odd) * (1 - 2 * core)
             return resident + (1 - 2 * bit(b)) * (1 << b)
 
-        lag = len(spans) if r == 0 else LAG
+        lag = len(spans) if r == 0 else 1 if bits - 1 in moves(r, bits) else LAG
         for q in range(len(spans) + lag):
             if q < len(spans):
                 cost(q)
-            if r == 0 and q == len(spans) - 1:
-                spread_all.wait()
-                for s in range(rounds):
-                    b = s % bits
-                    rows_v[s:s + 1, :] = (perms[2 * b + odd, s:s + 1, :] if b else
-                                          perms[1 - odd, s:s + 1, :]).astype(jnp.float32)
-                cols_v[...] = rows_v[...].T
-                hots(0)
             if q >= lag:
                 finish(q - lag)
 
         by_column = 1.0 / (1.0 + total_columns[0])
-        mix = (hot_r[...] + fourths[...] * by_column).astype(jnp.bfloat16).T
+        mix = (hot_r[r] + fourths[...] * by_column).astype(jnp.bfloat16).T
         for k in chunks:
             init[0, :, k] = merged(init[0, :, k], mix, visitor[:, k])
         pending += sum(sums, [])
@@ -212,7 +219,6 @@
                 pltpu.make_async_copy(dst, dst, out_recv.at[s]).wait()
         else:
             pending += onward
-            hots(r + 1)
     for copy in pending:
         copy.wait_send()
 
@@ -235,10 +241,11 @@
         away = 2 * (n_slab - 1)
         return pl.pallas_call(
             functools.partial(kernel, n_rep, n_slab, rounds, cuts),
-            out_shape=jax.ShapeDtypeStruct(weights.shape, weights.dtype),
-            in_specs=[pl.BlockSpec(memory_space=pltpu.VMEM)] * 2,
+            out_shape=pltpu.VMEM(weights.shape, weights.dtype),
+            in_specs=[pl.BlockSpec(memory_space=pl.ANY)] * 2,
             out_specs=pl.BlockSpec(memory_space=pltpu.VMEM),
             scratch_shapes=[
+                vmem(weights.shape, bf16), vmem(perms.shape, jnp.int32),
                 vmem((2, ffw, block), bf16),
                 vmem((rounds - 1, ffw, block), bf16),
                 vmem((rounds, ffw, block), bf16),
@@ -247,12 +254,12 @@
                 vmem((rounds, ffw, ffw), bf16),
                 vmem((rounds, away, ffw, ffw), bf16),
                 vmem((ffw, ffw), f32),
-                vmem((ffw, ffw), f32),
-                vmem((ffw, ffw), f32),
+                vmem((rounds, ffw, ffw), f32),
+                vmem((rounds, ffw, ffw), f32),
                 vmem((2 * bits, rounds, ffw), jnp.int32),
                 vmem((rounds, ffw), f32),
                 vmem((ffw, rounds), f32),
-                dma((n_slab, 2)), dma((n_slab, 2)),
+                dma((2,)), dma((n_slab, 2)), dma((n_slab, 2)),
                 dma((rounds, pieces)), dma((rounds, pieces)),
                 dma((rounds, pieces)), dma((rounds, pieces)),
                 dma((rounds, away, pieces)), dma((rounds, away, pieces)),

time: 136 us -> 132 us (0.971)
  Pallas kernels: 134 us -> 131 us
    pallas_call x1, Pallas kernels: 134 us -> 131 us  [local(): pl.pallas_call(functools.partial(kernel, n_rep, n_slab, rounds, cuts), ou...]
where the time goes in v2:
time: 132 us
  Pallas kernels  131 us (99%)
    pallas_call x1, Pallas kernels, local(): pl.pallas_call(functools.partial(kernel, n_rep, n_slab, rounds, cuts), ou...  131 us

profile of v2, /device:TPU:9, one launch (start us, length us, event | category | flops | bytes accessed | tf_op | source)
XLA Modules:
  0.0 132.2 jit_solution(14760180140524044391)
XLA Ops:
  0.0 131.3 %shard_map.28 = bf16[1,128,3072]{2,1,0:T(8,128)(2,1)S(1)} custom-call(bf16[1,128,3072]{2,1,0:T(8,128)(2,1)} %w_hbm.1, s32[1,8,256]{2,1,0:T(8,128)} %p_hbm.1), custom_call_target="tpu_custom_call" | custom-call | tf_op jit(solution)/shard_map/pallas_call | solution.py:242
  131.3 0.9 copy.4

commit v3 on v2

--- a/solution.py
+++ b/solution.py
@@ -9,7 +9,7 @@
 from jax.sharding import PartitionSpec as P
 
 CHUNK = 256
-PIECES = 4
+PARTS = 2
 LAG = 2
 
 
@@ -17,9 +17,9 @@
     return tuple(sorted(b for b in ((r - 1) % bits, r % bits) if b))
 
 
-def kernel(n_rep, n_slab, rounds, cuts, w_hbm, p_hbm, out_ref,
-           w_ref, p_ref, init, vis, sent, part, core_in, half_out, half_in, fourths, hot_v, hot_r, perms, rows_v, cols_v,
-           load, in_send, in_recv, ex_send, ex_recv, core_send, core_recv, half_send, half_recv,
+def kernel(n_rep, n_slab, rounds, parts, w_hbm, p_hbm, out_ref,
+           w_ref, p_ref, stage, init, vis, sent, part, core_in, half_out, half_in, fourths, hot_v, hot_r, perms, rows_v, cols_v,
+           load, give_send, give_recv, still_send, still_recv, first_send, first_recv, in_send, in_recv, ex_send, ex_recv, core_send, core_recv, half_send, half_recv,
            out_send, home_send, out_recv, perm_send, perm_recv):
     bits = n_rep.bit_length() - 1
     me = lax.axis_index("rep")
@@ -66,22 +66,59 @@
     for copy in loads:
         copy.wait()
 
-    firsts = []
-    rows_here = pl.ds(pl.multiple_of(slab * half, half), half)
-    for ds_ in list(range(1, n_slab)) + [0]:
-        for dc in range(2):
-            slab_to = (slab + ds_) % n_slab
-            core_to = core if dc == 0 else 1 - core
-            start = (slab_to * 2 + core_to) * block
-            src = w_ref.at[0, :, pl.ds(pl.multiple_of(start, 128), block)]
-            dst = init.at[odd, rows_here]
-            if ds_ == 0 and dc == 0:
-                copy = pltpu.make_async_copy(src, dst, in_recv.at[0, 0])
-            else:
-                copy = remote(src, dst, in_send.at[ds_, dc], in_recv.at[ds_, dc],
-                              me if dc == 0 else flipped(0), slab_to)
-            copy.start()
-            firsts.append(copy)
+    def columns_of(slab_at, core_at):
+        return pl.ds(pl.multiple_of((slab_at * 2 + core_at) * block, 128), block)
+
+    base = slab * half
+    rows_here = pl.ds(pl.multiple_of(base, half), half)
+    gives, stills, moved = [], [], [[] for _ in parts[1:]]
+    for ds_ in range(1, n_slab):
+        gives.append(remote(w_ref.at[0, :, columns_of((slab + ds_) % n_slab, 1 - core)], stage.at[ds_ - 1],
+                            give_send.at[ds_ - 1], give_recv.at[ds_ - 1], flipped(0), slab))
+        gives[-1].start()
+    own = pltpu.make_async_copy(w_ref.at[0, :, columns_of(slab, core)], init.at[odd, rows_here], first_recv.at[0])
+    beside = remote(w_ref.at[0, :, columns_of(slab, 1 - core)], init.at[odd, rows_here], first_send,
+                    first_recv.at[1], flipped(0), slab)
+
+    def crossing(ds_, src, kind, k):
+        slab_to = (slab + ds_) % n_slab
+        if kind == 0:
+            return remote(src, init.at[0, rows_here], still_send.at[ds_ - 1], still_recv.at[ds_ - 1], me, slab_to)
+        size = parts[k + 1] - parts[k]
+        dst = init.at[1, pl.ds(pl.multiple_of(base + parts[k], 16), size)]
+        return remote(src.at[pl.ds(parts[k], size)], dst, in_send.at[ds_ - 1, k], in_recv.at[ds_ - 1, k], me, slab_to)
+
+    def mine(ds_):
+        return w_ref.at[0, :, columns_of((slab + ds_) % n_slab, core)]
+
+    @pl.when(odd == 0)
+    def _():
+        for ds_ in range(1, n_slab):
+            crossing(ds_, mine(ds_), 0, 0).start()
+
+    own.start()
+    beside.start()
+    for copy in gives:
+        copy.wait_recv()
+
+    @pl.when(odd == 0)
+    def _():
+        for k in range(len(parts) - 1):
+            for ds_ in range(1, n_slab):
+                crossing(ds_, stage.at[ds_ - 1], 1, k).start()
+
+    @pl.when(odd == 1)
+    def _():
+        for ds_ in range(1, n_slab):
+            crossing(ds_, stage.at[ds_ - 1], 0, 0).start()
+        for k in range(len(parts) - 1):
+            for ds_ in range(1, n_slab):
+                crossing(ds_, mine(ds_), 1, k).start()
+
+    for ds_ in range(1, n_slab):
+        stills.append(crossing(ds_, stage.at[ds_ - 1], 0, 0))
+        for k in range(len(parts) - 1):
+            moved[k].append(crossing(ds_, stage.at[ds_ - 1], 1, k))
 
     perms[0] = p_ref[0]
     for b in range(bits):
@@ -100,7 +137,8 @@
         return ((own.astype(jnp.float32) + aligned) * (1.0 / math.sqrt(2.0))).astype(jnp.bfloat16)
 
     chunks = [pl.ds(k * CHUNK, CHUNK) for k in range(block // CHUNK)]
-    spans = [pl.ds(a, b - a) for a, b in zip(cuts[:-1], cuts[1:])]
+    cuts = [(h * half + a, h * half + b) for a, b in zip(parts[:-1], parts[1:]) for h in range(n_slab)]
+    spans = [pl.ds(a, b - a) for a, b in cuts]
     columns = lax.broadcasted_iota(jnp.int32, (ffw, ffw), 1)
     rows = lax.broadcasted_iota(jnp.int32, (ffw, ffw), 0)
 
@@ -112,10 +150,12 @@
     for r in range(rounds):
         hot_v[r] = (cols_v[:, r:r + 1].astype(jnp.int32) == columns).astype(jnp.float32)
         hot_r[r] = (perms[odd, r:r + 1, :] == rows).astype(jnp.float32)
-    for copy in firsts:
-        copy.wait()
-
-    pending = []
+    own.wait()
+    beside.wait_recv()
+    for copy in stills:
+        copy.wait_recv()
+
+    pending = gives + [beside] + stills + sum(moved, [])
     arrivals = None
     source = slab * 2 + core
     for r in range(rounds):
@@ -129,6 +169,9 @@
             its = spans[q]
             if r:
                 arrivals[q].wait_recv()
+            elif q % n_slab == 0:
+                for copy in moved[q // n_slab]:
+                    copy.wait_recv()
             partial = lax.dot_general(visitor[its, :], init[0], (((1,), (1,)), ((), ())),
                                       preferred_element_type=jnp.float32)
             part[r, its, :] = partial
@@ -160,8 +203,8 @@
             for k in chunks:
                 sent[r, its, k] = merged(visitor[its, k], mix, init[0, :, k])
             if last:
-                h = cuts[q] // half
-                dst = out_ref.at[0, pl.ds(cuts[q] - h * half, cuts[q + 1] - cuts[q]),
+                h = cuts[q][0] // half
+                dst = out_ref.at[0, pl.ds(cuts[q][0] - h * half, cuts[q][1] - cuts[q][0]),
                                  pl.ds(pl.multiple_of(source * block, 128), block)]
                 j = resident_flipped(r % bits)
                 copy = remote(sent.at[r, its], dst, out_send.at[q], out_recv.at[source], j, h)
@@ -232,20 +275,20 @@
         ffw = perms.shape[2]
         bits = n_rep.bit_length() - 1
         block = width // (2 * n_slab)
-        size = ffw // PIECES
-        cuts = list(range(0, ffw + 1, size))
-        pieces = len(cuts) - 1
+        parts = [k * half // PARTS for k in range(PARTS + 1)]
+        pieces = PARTS * n_slab
         vmem = pltpu.VMEM
         dma = pltpu.SemaphoreType.DMA
         bf16, f32 = jnp.bfloat16, jnp.float32
         away = 2 * (n_slab - 1)
         return pl.pallas_call(
-            functools.partial(kernel, n_rep, n_slab, rounds, cuts),
+            functools.partial(kernel, n_rep, n_slab, rounds, parts),
             out_shape=pltpu.VMEM(weights.shape, weights.dtype),
             in_specs=[pl.BlockSpec(memory_space=pl.ANY)] * 2,
             out_specs=pl.BlockSpec(memory_space=pltpu.VMEM),
             scratch_shapes=[
                 vmem(weights.shape, bf16), vmem(perms.shape, jnp.int32),
+                vmem((n_slab - 1, half, block), bf16),
                 vmem((2, ffw, block), bf16),
                 vmem((rounds - 1, ffw, block), bf16),
                 vmem((rounds, ffw, block), bf16),
@@ -259,7 +302,8 @@
                 vmem((2 * bits, rounds, ffw), jnp.int32),
                 vmem((rounds, ffw), f32),
                 vmem((ffw, rounds), f32),
-                dma((2,)), dma((n_slab, 2)), dma((n_slab, 2)),
+                dma((2,)), dma((n_slab - 1,)), dma((n_slab - 1,)), dma((n_slab - 1,)), dma((n_slab - 1,)),
+                dma, dma((2,)), dma((n_slab - 1, PARTS)), dma((n_slab - 1, PARTS)),
                 dma((rounds, pieces)), dma((rounds, pieces)),
                 dma((rounds, pieces)), dma((rounds, pieces)),
                 dma((rounds, away, pieces)), dma((rounds, away, pieces)),

time: 132 us -> 132 us (level)
  no operation moved by 1% of the time
where the time goes in v3:
time: 132 us
  Pallas kernels  131 us (99%)
    pallas_call x1, Pallas kernels, local(): pl.pallas_call(functools.partial(kernel, n_rep, n_slab, rounds, parts), o...  131 us

profile of v3, /device:TPU:9, one launch (start us, length us, event | category | flops | bytes accessed | tf_op | source)
XLA Modules:
  0.0 131.7 jit_solution(4336304544422533412)
XLA Ops:
  0.0 130.8 %shard_map.28 = bf16[1,128,3072]{2,1,0:T(8,128)(2,1)S(1)} custom-call(bf16[1,128,3072]{2,1,0:T(8,128)(2,1)} %w_hbm.1, s32[1,8,256]{2,1,0:T(8,128)} %p_hbm.1), custom_call_target="tpu_custom_call" | custom-call | tf_op jit(solution)/shard_map/pallas_call | solution.py:284
  130.8 0.9 copy.4

commit v4 on v3

--- a/solution.py
+++ b/solution.py
@@ -221,7 +221,7 @@
                 return me + (1 - odd) * (1 - 2 * core)
             return resident + (1 - 2 * bit(b)) * (1 << b)
 
-        lag = len(spans) if r == 0 else 1 if bits - 1 in moves(r, bits) else LAG
+        lag = len(spans) if r == 0 else 1 if r % bits and bits - 1 in moves(r, bits) + moves(r + 1, bits) else LAG
         for q in range(len(spans) + lag):
             if q < len(spans):
                 cost(q)

time: 132 us -> 131 us (level)
    pallas_call x1, Pallas kernels: 131 us -> 130 us  [local(): pl.pallas_call(functools.partial(kernel, n_rep, n_slab, rounds, parts), o...]
where the time goes in v4:
time: 131 us; the launch traced here: 130 us
  Pallas kernels  130 us (99%)
    pallas_call x1, Pallas kernels, local(): pl.pallas_call(functools.partial(kernel, n_rep, n_slab, rounds, parts), o...  130 us

profile of v4, /device:TPU:9, one launch (start us, length us, event | category | flops | bytes accessed | tf_op | source)
XLA Modules:
  0.0 130.4 jit_solution(12444263108506339181)
XLA Ops:
  0.0 129.5 %shard_map.28 = bf16[1,128,3072]{2,1,0:T(8,128)(2,1)S(1)} custom-call(bf16[1,128,3072]{2,1,0:T(8,128)(2,1)} %w_hbm.1, s32[1,8,256]{2,1,0:T(8,128)} %p_hbm.1), custom_call_target="tpu_custom_call" | custom-call | tf_op jit(solution)/shard_map/pallas_call | solution.py:284
  129.5 0.9 copy.4

commit v5 on v4

--- a/solution.py
+++ b/solution.py
@@ -179,18 +179,19 @@
             for ds_ in range(1, n_slab):
                 for dc in range(2):
                     at = 2 * (ds_ - 1) + dc
-                    sums[q].append(remote(half_out.at[r, its], half_in.at[r, at, its], half_send.at[r, at, q],
-                                          half_recv.at[r, at, q], me if dc == 0 else flipped(0),
+                    sums[q].append(remote(half_out.at[r, its], half_in.at[r, at, its], half_send,
+                                          half_recv.at[r, q], me if dc == 0 else flipped(0),
                                           (slab + ds_) % n_slab))
-            sums[q].append(remote(part.at[r, its], core_in.at[r, its], core_send.at[r, q], core_recv.at[r, q],
+            sums[q].append(remote(part.at[r, its], core_in.at[r, its], core_send, core_recv.at[r, q],
                                   flipped(0), slab))
             for copy in sums[q]:
                 copy.start()
 
         def finish(q):
             its = spans[q]
-            for copy in sums[q]:
-                copy.wait_recv()
+            both = half_in.at[r, :, its]
+            remote(both, both, half_send, half_recv.at[r, q], flipped(0), slab).wait_recv()
+            sums[q][-1].wait_recv()
             total = part[r, its, :] + core_in[r, its, :]
             for at in range(2 * (n_slab - 1)):
                 total = total + half_in[r, at, its, :].astype(jnp.float32)
@@ -207,9 +208,9 @@
                 dst = out_ref.at[0, pl.ds(cuts[q][0] - h * half, cuts[q][1] - cuts[q][0]),
                                  pl.ds(pl.multiple_of(source * block, 128), block)]
                 j = resident_flipped(r % bits)
-                copy = remote(sent.at[r, its], dst, out_send.at[q], out_recv.at[source], j, h)
+                copy = remote(sent.at[r, its], dst, out_send, out_recv.at[source], j, h)
             else:
-                copy = remote(sent.at[r, its], vis.at[r, its], ex_send.at[r, q], ex_recv.at[r, q],
+                copy = remote(sent.at[r, its], vis.at[r, its], ex_send, ex_recv.at[r, q],
                               flipped(*moves(r + 1, bits)), slab)
             copy.start()
             onward.append(copy)
@@ -232,7 +233,6 @@
         mix = (hot_r[r] + fourths[...] * by_column).astype(jnp.bfloat16).T
         for k in chunks:
             init[0, :, k] = merged(init[0, :, k], mix, visitor[:, k])
-        pending += sum(sums, [])
         arrivals = onward
         if last:
             for h in range(n_slab):
@@ -247,8 +247,10 @@
                 @pl.when(jnp.logical_not(stay))
                 def _():
                     remote(src, dst, home_send.at[h], out_recv.at[source], resident, h).start()
-            for copy in onward:
+            for copy in pending:
                 copy.wait_send()
+            for whole, sem in ((half_in, half_send), (core_in, core_send), (vis, ex_send), (sent.at[r], out_send)):
+                remote(whole, whole, sem, out_recv.at[0], flipped(0), slab).wait_send()
             for h in range(n_slab):
                 stay = jnp.logical_and(odd == 0, slab == h)
 
@@ -260,10 +262,6 @@
             for s in range(2 * n_slab):
                 dst = out_ref.at[0, :, pl.ds(s * block, block)]
                 pltpu.make_async_copy(dst, dst, out_recv.at[s]).wait()
-        else:
-            pending += onward
-    for copy in pending:
-        copy.wait_send()
 
 
 def solution(mesh):
@@ -304,10 +302,10 @@
                 vmem((ffw, rounds), f32),
                 dma((2,)), dma((n_slab - 1,)), dma((n_slab - 1,)), dma((n_slab - 1,)), dma((n_slab - 1,)),
                 dma, dma((2,)), dma((n_slab - 1, PARTS)), dma((n_slab - 1, PARTS)),
-                dma((rounds, pieces)), dma((rounds, pieces)),
-                dma((rounds, pieces)), dma((rounds, pieces)),
-                dma((rounds, away, pieces)), dma((rounds, away, pieces)),
-                dma((pieces,)), dma((n_slab,)), dma((2 * n_slab,)),
+                dma, dma((rounds - 1, pieces)),
+                dma, dma((rounds, pieces)),
+                dma, dma((rounds, pieces)),
+                dma, dma((n_slab,)), dma((2 * n_slab,)),
                 dma, dma,
             ],
             compiler_params=pltpu.CompilerParams(collective_id=0, has_side_effects=True, vmem_limit_bytes=60 * 1024 * 1024),

time: 131 us -> 129 us (0.985)
  Pallas kernels: 130 us -> 128 us
    pallas_call x1, Pallas kernels: 130 us -> 128 us  [local(): pl.pallas_call(functools.partial(kernel, n_rep, n_slab, rounds, parts), o...]
where the time goes in v5:
time: 129 us
  Pallas kernels  128 us (99%)
    pallas_call x1, Pallas kernels, local(): pl.pallas_call(functools.partial(kernel, n_rep, n_slab, rounds, parts), o...  128 us

profile of v5, /device:TPU:9, one launch (start us, length us, event | category | flops | bytes accessed | tf_op | source)
XLA Modules:
  0.0 128.7 jit_solution(3142456355509092997)
XLA Ops:
  0.0 127.8 %shard_map.28 = bf16[1,128,3072]{2,1,0:T(8,128)(2,1)S(1)} custom-call(bf16[1,128,3072]{2,1,0:T(8,128)(2,1)} %w_hbm.1, s32[1,8,256]{2,1,0:T(8,128)} %p_hbm.1), custom_call_target="tpu_custom_call" | custom-call | tf_op jit(solution)/shard_map/pallas_call | solution.py:282
  127.8 0.9 copy.4
